TPU v7x, 256 devices: a whole 4x4x8 slice. The times are simulated.
256 devices in a mesh: replica: 16 (over x_hi, z), tensor: 16 (over y, x_lo, core).
Axes of the slice: x: 4 (x_hi: 2, x_lo: 2; x = x_hi * 2 + x_lo), y: 4, z: 8, core: 2. Of those that a mesh axis runs over, the one named last changes fastest.
Arguments:
- hidden: bfloat16 [512, 8192], P('replica'), may hold values from -16 to 16
- q_weight: bfloat16 [8192, 4096], P(None, 'tensor'), may hold values from -0.0625 to 0.0625
- q_gain: float32 [128], replicated, may hold values from 0.1 to 1.9
- o_weight: bfloat16 [4096, 8192], P('tensor'), may hold values from -0.125 to 0.125
- attn_gate: float32 [1], replicated, may hold values from 0.5 to 1.5
- key_codes: bfloat16 [128, 512, 1024], P('replica', 'tensor'), may hold values from -96 to 96
- value_codes: bfloat16 [128, 512, 1024], P('replica', 'tensor'), may hold values from -96 to 96
- key_scales: bfloat16 [128, 16, 8], P('replica', 'tensor'), may hold values from 0.02 to 8
- value_scales: bfloat16 [128, 16, 8], P('replica', 'tensor'), may hold values from 0.019897461 to 0.119628906
- lengths: int32 [128], P('replica'), may hold values from 128 to 512
- dest_replica: int32 [16, 6], replicated, may hold values from 0 to 15, as said below
- move_slot: int32 [16, 6], P('replica'), may hold values from 0 to 7, as said below
Outputs:
- mixed: bfloat16 [512, 8192], P('replica', 'tensor')
- new_keys: bfloat16 [128, 512, 1024], P('replica', 'tensor')
- new_values: bfloat16 [128, 512, 1024], P('replica', 'tensor')
- new_key_scales: bfloat16 [128, 16, 8], P('replica', 'tensor')
- new_value_scales: bfloat16 [128, 16, 8], P('replica', 'tensor')
Inputs may be any that keep to these rules, and one draw needn't show every extreme that they name: For each j the column dest_replica[:, j] names every replica once, so each replica receives exactly 6 requests, at most one from each replica; a request may stay on its own replica. `move_slot`: the 6 slots of one replica are different.
All inputs are finite; a program needn't handle non-finite values.
Results may differ from a plain program's by a relative error of at most 0.0065.
Values may be sent and summed in bfloat16 or wider, within the bound.
No kernel may reach another device: no remote copies, remote signals or barrier semaphores. Data moves between devices by JAX's collectives and lax.ppermute only.
A program may use at most 64 MiB of HBM per device.

v0:
```python
import jax
import jax.numpy as jnp
from jax import lax
from jax.sharding import PartitionSpec as P

NEGATIVE = -1e30
EPSILON = 1e-06


def laid_out(tiles, dim):
    tiles = jnp.moveaxis(tiles, 0, dim)
    shape = tiles.shape
    return tiles.reshape(*shape[:dim], shape[dim] * shape[dim + 1], *shape[dim + 2 :])


def from_everyone(array, axis):
    copies = jnp.broadcast_to(array, (lax.axis_size(axis), *array.shape))
    return lax.all_to_all(copies, axis, split_axis=0, concat_axis=0, tiled=True)


def gather_directly(array, axis, dim):
    return laid_out(from_everyone(array, axis), dim)


def sent_together(arrays, axis, split_dim, concat_dim, along):
    columns = [a.reshape(*a.shape[:along], -1) for a in arrays]
    both = jnp.concatenate(columns, axis=along)
    result, at, done = (
        lax.all_to_all(both, axis, split_axis=split_dim, concat_axis=concat_dim, tiled=True),
        0,
        [],
    )
    for a, column in zip(arrays, columns):
        share = result[..., at : at + column.shape[along]]
        done.append(share.reshape(*share.shape[:along], *a.shape[along:]))
        at += column.shape[along]
    return tuple(done)


def cut_along(array, dim, count):
    before, after = (array.shape[:dim], array.shape[dim + 1 :])
    return jnp.moveaxis(array.reshape(*before, count, -1, *after), dim, 0)


def sent_and_summed(array, axis, dim):
    count = lax.axis_size(axis)
    tiles = lax.all_to_all(cut_along(array, dim, count), axis, 0, 0, tiled=True)
    return jnp.sum(tiles, axis=0)


def outgoing(send_table, codes):
    flat = codes.reshape(codes.shape[0], -1)
    moved = jnp.dot(send_table, flat, preferred_element_type=jnp.float32)
    return moved.astype(jnp.bfloat16).reshape((send_table.shape[0],) + codes.shape[1:])


def incoming(select, keep, received, codes):
    flat = received.reshape(received.shape[0], -1)
    placed = jnp.dot(select, flat, preferred_element_type=jnp.float32).astype(jnp.bfloat16)
    former = codes.reshape(codes.shape[0], -1)
    return jnp.where(keep[:, None], former, placed).reshape(codes.shape)


def attend(
    hidden,
    q_weight,
    q_gain,
    o_weight,
    attn_gate,
    key_codes,
    value_codes,
    key_scales,
    value_scales,
    lengths,
):
    tensors = lax.axis_size("tensor")
    rank = lax.axis_index("tensor")
    held, span, kv_width = key_codes.shape
    kv_heads = key_scales.shape[2]
    head_dim = kv_width // kv_heads
    rows = hidden.shape[0]
    drafts = rows // held
    local_heads = q_weight.shape[1] // head_dim
    projected = jnp.dot(hidden, q_weight, preferred_element_type=jnp.float32).reshape(
        rows, local_heads, head_dim
    )
    projected = projected * lax.rsqrt(
        jnp.mean(projected * projected, axis=-1, keepdims=True) + EPSILON
    )
    query = (projected * q_gain * head_dim ** (-0.5)).astype(jnp.bfloat16)
    every_head = gather_directly(query, "tensor", 1)
    heads = every_head.shape[1]
    grouped = every_head.reshape(held, drafts, kv_heads, heads // kv_heads, head_dim)
    keys = key_codes.reshape(held, span, kv_heads, head_dim)
    values = value_codes.reshape(held, span, kv_heads, head_dim)
    scores = jnp.einsum("rsngd,rtnd->rsngt", grouped, keys, preferred_element_type=jnp.float32)
    scores = scores * key_scales[:, 0, :].astype(jnp.float32)[:, None, :, None, None]
    position = rank * span + jnp.arange(span, dtype=jnp.int32)
    valid = (position[None, :] < lengths[:, None])[:, None, None, None, :]
    block_max = jnp.max(jnp.where(valid, scores, NEGATIVE), axis=-1)
    weights = jnp.where(valid, jnp.exp(scores - block_max[..., None]), 0.0)
    block_sum = jnp.sum(weights, axis=-1)
    block_out = jnp.einsum(
        "rsngt,rtnd->rsngd",
        weights.astype(jnp.bfloat16),
        values,
        preferred_element_type=jnp.float32,
    )
    block_out = block_out * value_scales[:, 0, :].astype(jnp.float32)[:, None, :, None, None]
    partial_value = (
        block_max.reshape(rows, heads),
        block_sum.reshape(rows, heads),
        block_out.reshape(rows, heads, head_dim),
    )
    peaks, totals, pieces = (
        lax.all_to_all(partial_value[0], "tensor", split_axis=1, concat_axis=0, tiled=True),
        *sent_together((partial_value[1], partial_value[2]), "tensor", 1, 0, 2),
    )
    peaks = peaks.reshape(tensors, rows, local_heads)
    top = jnp.max(peaks, axis=0)
    factor = jnp.exp(peaks - top[None])
    total = jnp.sum(totals.reshape(tensors, rows, local_heads) * factor, axis=0)
    summed = jnp.sum(
        pieces.reshape(tensors, rows, local_heads, head_dim) * factor[..., None], axis=0
    )
    attended = (
        (summed / total[..., None]).astype(jnp.bfloat16).reshape(rows, local_heads * head_dim)
    )
    terms = jnp.dot(attended, o_weight, preferred_element_type=jnp.float32)
    shares = sent_and_summed(terms, "tensor", 1)
    width = shares.shape[1]
    residual = lax.dynamic_slice_in_dim(hidden, rank * width, width, 1).astype(jnp.float32)
    return (residual + jnp.tanh(attn_gate[0]) * shares).astype(jnp.bfloat16)


def local(
    hidden,
    q_weight,
    q_gain,
    o_weight,
    attn_gate,
    key_codes,
    value_codes,
    key_scales,
    value_scales,
    lengths,
    dest_replica,
    move_slot,
):
    replicas = lax.axis_size("replica")
    here = lax.axis_index("replica")
    held = key_codes.shape[0]
    slots = move_slot[0]
    own_dest = lax.dynamic_index_in_dim(dest_replica, here, 0, keepdims=False)
    replica_ids = jnp.arange(replicas, dtype=jnp.int32)
    slot_ids = jnp.arange(held, dtype=jnp.int32)
    slot_match = slots[:, None] == slot_ids[None, :]
    send_table = jnp.any(
        (own_dest[:, None, None] == replica_ids[None, :, None]) & slot_match[:, None, :], axis=0
    ).astype(jnp.bfloat16)
    arrive = dest_replica == here
    select = jnp.any(slot_match.T[:, None, :] & arrive[None, :, :], axis=2).astype(jnp.bfloat16)
    keep = jnp.logical_not(jnp.any(slot_match, axis=0))
    received = sent_together(
        (
            outgoing(send_table, key_codes),
            outgoing(send_table, value_codes),
            outgoing(send_table, key_scales),
            outgoing(send_table, value_scales),
        ),
        "replica",
        0,
        0,
        1,
    )
    new_keys = incoming(select, keep, received[0], key_codes)
    new_values = incoming(select, keep, received[1], value_codes)
    new_key_scales = incoming(select, keep, received[2], key_scales)
    new_value_scales = incoming(select, keep, received[3], value_scales)
    mixed = attend(
        hidden,
        q_weight,
        q_gain,
        o_weight,
        attn_gate,
        key_codes,
        value_codes,
        key_scales,
        value_scales,
        lengths,
    )
    return (mixed, new_keys, new_values, new_key_scales, new_value_scales)


def solution(mesh):
    return jax.shard_map(
        local,
        mesh=mesh,
        in_specs=(
            P("replica", None),
            P(None, "tensor"),
            P(),
            P("tensor", None),
            P(),
            P("replica", "tensor", None),
            P("replica", "tensor", None),
            P("replica", "tensor", None),
            P("replica", "tensor", None),
            P("replica"),
            P(),
            P("replica", None),
        ),
        out_specs=(
            P("replica", "tensor"),
            P("replica", "tensor", None),
            P("replica", "tensor", None),
            P("replica", "tensor", None),
            P("replica", "tensor", None),
        ),
        check_vma=False,
    )
```

profile of v0, /device:TPU:32, one launch (start us, length us, event | category | flops | bytes accessed | tf_op | source)
XLA Modules:
  0.0 155.7 jit_solution(13727029361715227020)
XLA Ops:
  0.7 3.2 %fusion.35 = f32[32,256]{1,0:T(8,128)S(1)} fusion(bf16[32,8192]{1,0:T(8,128)(2,1)} %param.12, bf16[8192,256]{1,0:T(8,128)(2,1)} %param.13), kind=kOutput, calls=%fused_computation.72 | convolution fusion | flops 134217728 | bytes 4751360 | tf_op jit(solution)/shard_map/dot_general | solution.py:84
  5.0 5.5 %all-to-all-start = ((bf16[16,32,2,128]{3,1,2,0:T(8,128)(2,1)}), bf16[16,32,2,128]{3,1,2,0:T(8,128)(2,1)S(1)}, u32[]{:S(2)}, u32[]{:S(2)}) async-start(bf16[16,32,2,128]{3,1,2,0:T(8,128)(2,1)} %broadcast_in_dim.65), calls=%async_computation | async-start | bytes 524288 | tf_op jit(solution)/shard_map/all_to_all | solution.py:18
  11.0 7.6 %all-to-all-done = bf16[16,32,2,128]{3,1,2,0:T(8,128)(2,1)S(1)} async-done(((bf16[16,32,2,128]{3,1,2,0:T(8,128)(2,1)}), bf16[16,32,2,128]{3,1,2,0:T(8,128)(2,1)S(1)}, u32[]{:S(2)}, u32[]{:S(2)}) %all-to-all-start) | async-done | bytes 262176 | tf_op jit(solution)/shard_map/all_to_all | solution.py:18
  19.1 0.8 fusion.15
  21.1 1.6 %copy.145 = f32[32,32,129]{2,0,1:T(8,128)} copy(f32[32,32,129]{2,1,0:T(8,128)S(1)} %pad_maximum_fusion) | data formatting | bytes 1056768 | tf_op jit(solution)/shard_map/concatenate | solution.py:27
  22.7 3.7 %all-to-all-start.1 = ((f32[32,32,129]{2,0,1:T(8,128)}), f32[32,32,129]{2,0,1:T(8,128)S(1)}, u32[]{:S(2)}, u32[]{:S(2)}) async-start(f32[32,32,129]{2,0,1:T(8,128)} %copy.145), calls=%async_computation.1 | async-start | bytes 2097152 | tf_op jit(solution)/shard_map/all_to_all | solution.py:29
  26.4 6.4 %copy.163 = bf16[8192,256]{1,0:T(8,128)(2,1)} copy(bf16[8192,256]{0,1:T(8,128)(2,1)} %bitcast.112) | data formatting | bytes 8388608 | tf_op jit(solution)/shard_map/dot_general | solution.py:129
  34.4 8.5 %all-to-all-done.1 = f32[32,32,129]{2,0,1:T(8,128)S(1)} async-done(((f32[32,32,129]{2,0,1:T(8,128)}), f32[32,32,129]{2,0,1:T(8,128)S(1)}, u32[]{:S(2)}, u32[]{:S(2)}) %all-to-all-start.1) | async-done | bytes 528416 | tf_op jit(solution)/shard_map/all_to_all | solution.py:29
  42.9 3.5 %all-to-all-start.2 = ((f32[32,16,2]{0,2,1:T(2,128)}), f32[32,16,2]{0,2,1:T(2,128)S(1)}, u32[]{:S(2)}, u32[]{:S(2)}) async-start(f32[32,16,2]{0,2,1:T(2,128)} %all_to_all.44), calls=%async_computation.2 | async-start | bytes 32768 | tf_op jit(solution)/shard_map/all_to_all | solution.py:116
  46.9 5.4 %all-to-all-done.2 = f32[32,16,2]{0,2,1:T(2,128)S(1)} async-done(((f32[32,16,2]{0,2,1:T(2,128)}), f32[32,16,2]{0,2,1:T(2,128)S(1)}, u32[]{:S(2)}, u32[]{:S(2)}) %all-to-all-start.2) | async-done | bytes 4128 | tf_op jit(solution)/shard_map/all_to_all | solution.py:116
  52.8 4.5 %convolution_bitcast_fusion = f32[16,32,512]{2,1,0:T(8,128)} fusion(bf16[32,256,1]{1,0,2:T(8,128)(2,1)S(1)} %reshape.208, bf16[16,512,256]{2,1,0:T(8,128)(2,1)} %bitcast.102), kind=kOutput, calls=%fused_computation.9 | convolution fusion | flops 134217728 | bytes 5259264 | tf_op jit(solution)/shard_map/dot_general | solution.py:129
  57.3 4.4 %all-to-all-start.3 = ((f32[16,32,512]{2,1,0:T(8,128)}), f32[16,32,512]{2,1,0:T(8,128)}, u32[]{:S(2)}, u32[]{:S(2)}) async-start(f32[16,32,512]{2,1,0:T(8,128)} %convolution_bitcast_fusion), calls=%async_computation.3 | async-start | bytes 2097152 | tf_op jit(solution)/shard_map/all_to_all | solution.py:47
  64.3 1.4 copy-done
  66.1 3.9 %reduce.4 = bf16[16,65552]{1,0:T(8,128)(2,1)S(1)} reduce(bf16[16,1,65552]{2,0,1:T(8,128)(2,1)} %bitcast.107, bf16[]{:T(256)} %broadcast.80), dimensions={1}, to_apply=%copy.154.reduce_sub_computation | reduce | bytes 4195330 | tf_op jit(solution)/shard_map/all_to_all | solution.py:29
  70.0 2.5 %reshape.212 = bf16[16,2,32776]{2,1,0:T(2,128)(2,1)} reshape(bf16[16,65552]{1,0:T(8,128)(2,1)S(1)} %reduce.4) | data formatting | bytes 4195328
  72.5 5.7 %all-to-all-done.3 = f32[16,32,512]{2,1,0:T(8,128)} async-done(((f32[16,32,512]{2,1,0:T(8,128)}), f32[16,32,512]{2,1,0:T(8,128)}, u32[]{:S(2)}, u32[]{:S(2)}) %all-to-all-start.3) | async-done | bytes 1048608 | tf_op jit(solution)/shard_map/all_to_all | solution.py:47
  78.2 10.7 %all-to-all-start.4 = ((bf16[16,2,32776]{2,1,0:T(2,128)(2,1)}), bf16[16,2,32776]{2,1,0:T(2,128)(2,1)S(1)}, u32[]{:S(2)}, u32[]{:S(2)}) async-start(bf16[16,2,32776]{2,1,0:T(2,128)(2,1)} %reshape.212), calls=%async_computation.4 | async-start | bytes 4210688 | tf_op jit(solution)/shard_map/all_to_all | solution.py:29
  89.8 1.3 reduce_sum.49
  91.1 1.4 add_convert_fusion
  92.5 46.7 %all-to-all-done.4 = bf16[16,2,32776]{2,1,0:T(2,128)(2,1)S(1)} async-done(((bf16[16,2,32776]{2,1,0:T(2,128)(2,1)}), bf16[16,2,32776]{2,1,0:T(2,128)(2,1)S(1)}, u32[]{:S(2)}, u32[]{:S(2)}) %all-to-all-start.4) | async-done | bytes 2097696 | tf_op jit(solution)/shard_map/all_to_all | solution.py:29
  139.2 9.9 %reshape.213 = bf16[16,1,65552]{2,1,0:T(2,128)(2,1)} reshape(bf16[16,2,32776]{2,1,0:T(2,128)(2,1)S(1)} %all-to-all-done.4) | data formatting | bytes 4195328
  149.1 2.4 %copy.190 = bf16[16,1,65552]{2,0,1:T(8,128)(2,1)S(1)} copy(bf16[16,1,65552]{2,1,0:T(2,128)(2,1)} %reshape.213) | data formatting | bytes 4195328
  153.6 1.1 copy.156
  154.7 1.1 copy.155
  (71 shorter events, 11.0 us)
Async XLA Ops:
  0.6 3.5 %copy-start.6 = (f32[128]{0:T(128)S(1)}, f32[128]{0:T(128)}, u32[]{:S(2)}) copy-start(f32[128]{0:T(128)} %param.14) | copy-start | bytes 1540
  0.6 9.9 %copy-start.5 = (bf16[8,1,8]{2,0,1:T(8,128)(2,1)S(1)}, bf16[8,1,8]{2,0,1:T(8,128)(2,1)}, u32[]{:S(2)}) copy-start(bf16[8,1,8]{2,0,1:T(8,128)(2,1)} %param.19) | copy-start | bytes 388
  0.7 9.9 %copy-start.4 = (bf16[8,1,8]{2,0,1:T(8,128)(2,1)S(1)}, bf16[8,1,8]{2,0,1:T(8,128)(2,1)}, u32[]{:S(2)}) copy-start(bf16[8,1,8]{2,0,1:T(8,128)(2,1)} %param.20) | copy-start | bytes 388
  0.7 9.9 %copy-start.1 = (bf16[8,32,1024]{2,1,0:T(8,128)(2,1)S(1)}, bf16[8,32,1024]{2,1,0:T(8,128)(2,1)}, u32[]{:S(2)}) copy-start(bf16[8,32,1024]{2,1,0:T(8,128)(2,1)} %param.18) | copy-start | bytes 1572868
  3.9 6.8 %copy-start.2 = (bf16[8,32,1024]{2,1,0:T(8,128)(2,1)S(1)}, bf16[8,32,1024]{2,1,0:T(8,128)(2,1)}, u32[]{:S(2)}) copy-start(bf16[8,32,1024]{2,1,0:T(8,128)(2,1)} %param.17) | copy-start | bytes 1572868
  3.9 6.9 %copy-start.7 = (s32[8]{0:T(128)S(1)}, s32[8]{0:T(128)}, u32[]{:S(2)}) copy-start(s32[8]{0:T(128)} %param.21) | copy-start | bytes 100
  5.0 13.5 %all-to-all-start = ((bf16[16,32,2,128]{3,1,2,0:T(8,128)(2,1)}), bf16[16,32,2,128]{3,1,2,0:T(8,128)(2,1)S(1)}, u32[]{:S(2)}, u32[]{:S(2)}) async-start(bf16[16,32,2,128]{3,1,2,0:T(8,128)(2,1)} %broadcast_in_dim.65), calls=%async_computation | async-start | bytes 524288 | tf_op jit(solution)/shard_map/all_to_all | solution.py:18
  22.7 20.2 %all-to-all-start.1 = ((f32[32,32,129]{2,0,1:T(8,128)}), f32[32,32,129]{2,0,1:T(8,128)S(1)}, u32[]{:S(2)}, u32[]{:S(2)}) async-start(f32[32,32,129]{2,0,1:T(8,128)} %copy.145), calls=%async_computation.1 | async-start | bytes 2097152 | tf_op jit(solution)/shard_map/all_to_all | solution.py:29
  26.4 6.4 %copy-start.3 = (s32[16,6]{0,1:T(8,128)S(1)}, s32[16,6]{0,1:T(8,128)}, u32[]{:S(2)}) copy-start(s32[16,6]{0,1:T(8,128)} %param.22) | copy-start | bytes 1156
  26.4 6.7 %copy-start.8 = (s32[1,6]{1,0:T(1,128)S(1)}, s32[1,6]{1,0:T(1,128)}, u32[]{:S(2)}) copy-start(s32[1,6]{1,0:T(1,128)} %param.23) | copy-start | bytes 76
  42.9 9.5 %all-to-all-start.2 = ((f32[32,16,2]{0,2,1:T(2,128)}), f32[32,16,2]{0,2,1:T(2,128)S(1)}, u32[]{:S(2)}, u32[]{:S(2)}) async-start(f32[32,16,2]{0,2,1:T(2,128)} %all_to_all.44), calls=%async_computation.2 | async-start | bytes 32768 | tf_op jit(solution)/shard_map/all_to_all | solution.py:116
  57.3 20.9 %all-to-all-start.3 = ((f32[16,32,512]{2,1,0:T(8,128)}), f32[16,32,512]{2,1,0:T(8,128)}, u32[]{:S(2)}, u32[]{:S(2)}) async-start(f32[16,32,512]{2,1,0:T(8,128)} %convolution_bitcast_fusion), calls=%async_computation.3 | async-start | bytes 2097152 | tf_op jit(solution)/shard_map/all_to_all | solution.py:47
  64.3 1.4 copy-start
  78.2 61.0 %all-to-all-start.4 = ((bf16[16,2,32776]{2,1,0:T(2,128)(2,1)}), bf16[16,2,32776]{2,1,0:T(2,128)(2,1)S(1)}, u32[]{:S(2)}, u32[]{:S(2)}) async-start(bf16[16,2,32776]{2,1,0:T(2,128)(2,1)} %reshape.212), calls=%async_computation.4 | async-start | bytes 4210688 | tf_op jit(solution)/shard_map/all_to_all | solution.py:29
where the time goes:
time: 157 us; the launch traced here: 156 us
  waiting for transfers between devices  73.9 us (47%)
  local copies, waits for them, and re-layouts  31.4 us (20%)
  starting transfers between devices  27.7 us (18%)
  matrix products  12.2 us (8%)
  other arithmetic  8.71 us (6%)
  between operations  1.72 us (1%)
    all_to_all x2, waiting for transfers between devices, sent_together(): lax.all_to_all(both, axis, split_axis=split_dim, concat_axis=concat_dim,...  55.2 us
    unnamed x28, local copies, waits for them, and re-layouts  19.3 us
    all_to_all x2, starting transfers between devices, sent_together(): lax.all_to_all(both, axis, split_axis=split_dim, concat_axis=concat_dim,...  14.4 us
    all_to_all x1, waiting for transfers between devices, from_everyone(): return lax.all_to_all(copies, axis, split_axis=0, concat_axis=0, tiled=True)  7.57 us
    dot_general x1, local copies, waits for them, and re-layouts, attend(): terms = jnp.dot(attended, o_weight, preferred_element_type=jnp.float32)  6.4 us
    all_to_all x1, waiting for transfers between devices, sent_and_summed(): tiles = lax.all_to_all(cut_along(array, dim, count), axis, 0, 0, tiled=True)  5.73 us
    all_to_all x1, starting transfers between devices, from_everyone(): return lax.all_to_all(copies, axis, split_axis=0, concat_axis=0, tiled=True)  5.5 us
    all_to_all x1, waiting for transfers between devices, attend(): lax.all_to_all(partial_value[0], 'tensor', split_axis=1, concat_axis=0, t...  5.44 us
  transfers between devices with their start and end apart: 5, of which 5 were waited for; matrix products, arithmetic and copies ran while one was open for 13% of the time, Pallas kernels for 0%

commit v1 on v0

--- a/solution.py
+++ b/solution.py
@@ -113,7 +113,15 @@
         block_out.reshape(rows, heads, head_dim),
     )
     peaks, totals, pieces = (
-        lax.all_to_all(partial_value[0], "tensor", split_axis=1, concat_axis=0, tiled=True),
+        jnp.concatenate(
+            lax.all_to_all(
+                jnp.stack(jnp.split(partial_value[0], lax.axis_size("tensor"), axis=1)),
+                "tensor",
+                0,
+                0,
+            ),
+            axis=0,
+        ),
         *sent_together((partial_value[1], partial_value[2]), "tensor", 1, 0, 2),
     )
     peaks = peaks.reshape(tensors, rows, local_heads)

time: 157 us -> 166 us (1.057)
  local copies, waits for them, and re-layouts: 31.4 us -> 40.7 us
    unnamed x28 -> x43, local copies, waits for them, and re-layouts: 19.3 us -> 27.8 us
where the time goes in v1:
time: 166 us; the launch traced here: 165 us
  waiting for transfers between devices  73.6 us (44%)
  local copies, waits for them, and re-layouts  40.7 us (25%)
  starting transfers between devices  27.8 us (17%)
  matrix products  12.2 us (7%)
  other arithmetic  8.7 us (5%)
  between operations  1.75 us (1%)
    all_to_all x2, waiting for transfers between devices, sent_together(): lax.all_to_all(both, axis, split_axis=split_dim, concat_axis=concat_dim,...  56.4 us
    unnamed x43, local copies, waits for them, and re-layouts  27.8 us
    all_to_all x2, starting transfers between devices, sent_together(): lax.all_to_all(both, axis, split_axis=split_dim, concat_axis=concat_dim,...  14.4 us
    all_to_all x1, waiting for transfers between devices, from_everyone(): return lax.all_to_all(copies, axis, split_axis=0, concat_axis=0, tiled=True)  7.57 us
    dot_general x1, local copies, waits for them, and re-layouts, attend(): terms = jnp.dot(attended, o_weight, preferred_element_type=jnp.float32)  6.4 us
    all_to_all x1, waiting for transfers between devices, sent_and_summed(): tiles = lax.all_to_all(cut_along(array, dim, count), axis, 0, 0, tiled=True)  5.73 us
    all_to_all x1, starting transfers between devices, from_everyone(): return lax.all_to_all(copies, axis, split_axis=0, concat_axis=0, tiled=True)  5.5 us
    dot_general x1, matrix products, attend(): terms = jnp.dot(attended, o_weight, preferred_element_type=jnp.float32)  4.49 us
  transfers between devices with their start and end apart: 5, of which 5 were waited for; matrix products, arithmetic and copies ran while one was open for 13% of the time, Pallas kernels for 0%

profile of v1, /device:TPU:32, one launch (start us, length us, event | category | flops | bytes accessed | tf_op | source)
XLA Modules:
  0.0 164.8 jit_solution(12785828334617476455)
XLA Ops:
  0.7 3.2 %fusion.33 = f32[32,256]{1,0:T(8,128)S(1)} fusion(bf16[32,8192]{1,0:T(8,128)(2,1)} %param.12, bf16[8192,256]{1,0:T(8,128)(2,1)} %param.13), kind=kOutput, calls=%fused_computation.84 | convolution fusion | flops 134217728 | bytes 4751360 | tf_op jit(solution)/shard_map/dot_general | solution.py:84
  5.0 5.5 %all-to-all-start = ((bf16[16,32,2,128]{3,1,2,0:T(8,128)(2,1)}), bf16[16,32,2,128]{3,1,2,0:T(8,128)(2,1)S(1)}, u32[]{:S(2)}, u32[]{:S(2)}) async-start(bf16[16,32,2,128]{3,1,2,0:T(8,128)(2,1)} %broadcast_in_dim.65), calls=%async_computation | async-start | bytes 524288 | tf_op jit(solution)/shard_map/all_to_all | solution.py:18
  11.0 7.6 %all-to-all-done = bf16[16,32,2,128]{3,1,2,0:T(8,128)(2,1)S(1)} async-done(((bf16[16,32,2,128]{3,1,2,0:T(8,128)(2,1)}), bf16[16,32,2,128]{3,1,2,0:T(8,128)(2,1)S(1)}, u32[]{:S(2)}, u32[]{:S(2)}) %all-to-all-start) | async-done | bytes 262176 | tf_op jit(solution)/shard_map/all_to_all | solution.py:18
  31.2 3.5 %all-to-all-start.2 = ((f32[16,32,2]{1,2,0:T(2,128)}), f32[16,32,2]{1,2,0:T(2,128)S(1)}, u32[]{:S(2)}, u32[]{:S(2)}) async-start(f32[16,32,2]{1,2,0:T(2,128)} %constant_dynamic-update-slice_fusion), calls=%async_computation.2 | async-start | bytes 32768 | tf_op jit(solution)/shard_map/all_to_all | solution.py:117
  35.2 1.6 copy.273
  36.8 3.9 %all-to-all-done.2 = f32[16,32,2]{1,2,0:T(2,128)S(1)} async-done(((f32[16,32,2]{1,2,0:T(2,128)}), f32[16,32,2]{1,2,0:T(2,128)S(1)}, u32[]{:S(2)}, u32[]{:S(2)}) %all-to-all-start.2) | async-done | bytes 4128 | tf_op jit(solution)/shard_map/all_to_all | solution.py:117
  40.7 3.7 %all-to-all-start.1 = ((f32[32,32,129]{2,0,1:T(8,128)}), f32[32,32,129]{2,0,1:T(8,128)S(1)}, u32[]{:S(2)}, u32[]{:S(2)}) async-start(f32[32,32,129]{2,0,1:T(8,128)} %copy.273), calls=%async_computation.1 | async-start | bytes 2097152 | tf_op jit(solution)/shard_map/all_to_all | solution.py:29
  44.4 6.4 %copy.307 = bf16[8192,256]{1,0:T(8,128)(2,1)} copy(bf16[8192,256]{0,1:T(8,128)(2,1)} %bitcast.132) | data formatting | bytes 8388608 | tf_op jit(solution)/shard_map/dot_general | solution.py:137
  51.2 9.7 %all-to-all-done.1 = f32[32,32,129]{2,0,1:T(8,128)S(1)} async-done(((f32[32,32,129]{2,0,1:T(8,128)}), f32[32,32,129]{2,0,1:T(8,128)S(1)}, u32[]{:S(2)}, u32[]{:S(2)}) %all-to-all-start.1) | async-done | bytes 528416 | tf_op jit(solution)/shard_map/all_to_all | solution.py:29
  61.8 4.5 %convolution_bitcast_fusion = f32[16,32,512]{2,1,0:T(8,128)} fusion(bf16[32,256,1]{1,0,2:T(8,128)(2,1)S(1)} %reshape.205, bf16[16,512,256]{2,1,0:T(8,128)(2,1)} %bitcast.122), kind=kOutput, calls=%fused_computation.9 | convolution fusion | flops 134217728 | bytes 5259264 | tf_op jit(solution)/shard_map/dot_general | solution.py:137
  66.3 4.4 %all-to-all-start.3 = ((f32[16,32,512]{2,1,0:T(8,128)}), f32[16,32,512]{2,1,0:T(8,128)}, u32[]{:S(2)}, u32[]{:S(2)}) async-start(f32[16,32,512]{2,1,0:T(8,128)} %convolution_bitcast_fusion), calls=%async_computation.3 | async-start | bytes 2097152 | tf_op jit(solution)/shard_map/all_to_all | solution.py:47
  73.3 1.4 copy-done
  75.1 3.9 %reduce.4 = bf16[16,65552]{1,0:T(8,128)(2,1)S(1)} reduce(bf16[16,1,65552]{2,0,1:T(8,128)(2,1)} %bitcast.127, bf16[]{:T(256)} %broadcast.80), dimensions={1}, to_apply=%copy.298.reduce_sub_computation | reduce | bytes 4195330 | tf_op jit(solution)/shard_map/all_to_all | solution.py:29
  79.0 2.5 %reshape.209 = bf16[16,2,32776]{2,1,0:T(2,128)(2,1)} reshape(bf16[16,65552]{1,0:T(8,128)(2,1)S(1)} %reduce.4) | data formatting | bytes 4195328
  81.5 5.7 %all-to-all-done.3 = f32[16,32,512]{2,1,0:T(8,128)} async-done(((f32[16,32,512]{2,1,0:T(8,128)}), f32[16,32,512]{2,1,0:T(8,128)}, u32[]{:S(2)}, u32[]{:S(2)}) %all-to-all-start.3) | async-done | bytes 1048608 | tf_op jit(solution)/shard_map/all_to_all | solution.py:47
  87.2 10.8 %all-to-all-start.4 = ((bf16[16,2,32776]{2,1,0:T(2,128)(2,1)}), bf16[16,2,32776]{2,1,0:T(2,128)(2,1)S(1)}, u32[]{:S(2)}, u32[]{:S(2)}) async-start(bf16[16,2,32776]{2,1,0:T(2,128)(2,1)} %reshape.209), calls=%async_computation.4 | async-start | bytes 4210688 | tf_op jit(solution)/shard_map/all_to_all | solution.py:29
  98.8 1.3 reduce_sum.49
  100.1 1.4 add_convert_fusion
  101.5 46.7 %all-to-all-done.4 = bf16[16,2,32776]{2,1,0:T(2,128)(2,1)S(1)} async-done(((bf16[16,2,32776]{2,1,0:T(2,128)(2,1)}), bf16[16,2,32776]{2,1,0:T(2,128)(2,1)S(1)}, u32[]{:S(2)}, u32[]{:S(2)}) %all-to-all-start.4) | async-done | bytes 2097696 | tf_op jit(solution)/shard_map/all_to_all | solution.py:29
  148.2 9.9 %reshape.210 = bf16[16,1,65552]{2,1,0:T(2,128)(2,1)} reshape(bf16[16,2,32776]{2,1,0:T(2,128)(2,1)S(1)} %all-to-all-done.4) | data formatting | bytes 4195328
  158.1 2.4 %copy.331 = bf16[16,1,65552]{2,0,1:T(8,128)(2,1)S(1)} copy(bf16[16,1,65552]{2,1,0:T(2,128)(2,1)} %reshape.210) | data formatting | bytes 4195328
  161.1 0.8 fusion.9
  162.6 1.1 copy.300
  163.7 1.1 copy.299
  (105 shorter events, 20.3 us)
Async XLA Ops:
  0.6 3.5 %copy-start.6 = (f32[128]{0:T(128)S(1)}, f32[128]{0:T(128)}, u32[]{:S(2)}) copy-start(f32[128]{0:T(128)} %param.14) | copy-start | bytes 1540
  0.6 9.9 %copy-start.5 = (bf16[8,1,8]{2,0,1:T(8,128)(2,1)S(1)}, bf16[8,1,8]{2,0,1:T(8,128)(2,1)}, u32[]{:S(2)}) copy-start(bf16[8,1,8]{2,0,1:T(8,128)(2,1)} %param.19) | copy-start | bytes 388
  0.7 9.9 %copy-start.4 = (bf16[8,1,8]{2,0,1:T(8,128)(2,1)S(1)}, bf16[8,1,8]{2,0,1:T(8,128)(2,1)}, u32[]{:S(2)}) copy-start(bf16[8,1,8]{2,0,1:T(8,128)(2,1)} %param.20) | copy-start | bytes 388
  0.7 9.9 %copy-start.1 = (bf16[8,32,1024]{2,1,0:T(8,128)(2,1)S(1)}, bf16[8,32,1024]{2,1,0:T(8,128)(2,1)}, u32[]{:S(2)}) copy-start(bf16[8,32,1024]{2,1,0:T(8,128)(2,1)} %param.18) | copy-start | bytes 1572868
  3.9 6.8 %copy-start.2 = (bf16[8,32,1024]{2,1,0:T(8,128)(2,1)S(1)}, bf16[8,32,1024]{2,1,0:T(8,128)(2,1)}, u32[]{:S(2)}) copy-start(bf16[8,32,1024]{2,1,0:T(8,128)(2,1)} %param.17) | copy-start | bytes 1572868
  3.9 6.9 %copy-start.7 = (s32[8]{0:T(128)S(1)}, s32[8]{0:T(128)}, u32[]{:S(2)}) copy-start(s32[8]{0:T(128)} %param.21) | copy-start | bytes 100
  5.0 13.5 %all-to-all-start = ((bf16[16,32,2,128]{3,1,2,0:T(8,128)(2,1)}), bf16[16,32,2,128]{3,1,2,0:T(8,128)(2,1)S(1)}, u32[]{:S(2)}, u32[]{:S(2)}) async-start(bf16[16,32,2,128]{3,1,2,0:T(8,128)(2,1)} %broadcast_in_dim.65), calls=%async_computation | async-start | bytes 524288 | tf_op jit(solution)/shard_map/all_to_all | solution.py:18
  31.2 9.5 %all-to-all-start.2 = ((f32[16,32,2]{1,2,0:T(2,128)}), f32[16,32,2]{1,2,0:T(2,128)S(1)}, u32[]{:S(2)}, u32[]{:S(2)}) async-start(f32[16,32,2]{1,2,0:T(2,128)} %constant_dynamic-update-slice_fusion), calls=%async_computation.2 | async-start | bytes 32768 | tf_op jit(solution)/shard_map/all_to_all | solution.py:117
  40.7 20.2 %all-to-all-start.1 = ((f32[32,32,129]{2,0,1:T(8,128)}), f32[32,32,129]{2,0,1:T(8,128)S(1)}, u32[]{:S(2)}, u32[]{:S(2)}) async-start(f32[32,32,129]{2,0,1:T(8,128)} %copy.273), calls=%async_computation.1 | async-start | bytes 2097152 | tf_op jit(solution)/shard_map/all_to_all | solution.py:29
  44.3 6.4 %copy-start.3 = (s32[16,6]{0,1:T(8,128)S(1)}, s32[16,6]{0,1:T(8,128)}, u32[]{:S(2)}) copy-start(s32[16,6]{0,1:T(8,128)} %param.22) | copy-start | bytes 1156
  44.4 6.7 %copy-start.8 = (s32[1,6]{1,0:T(1,128)S(1)}, s32[1,6]{1,0:T(1,128)}, u32[]{:S(2)}) copy-start(s32[1,6]{1,0:T(1,128)} %param.23) | copy-start | bytes 76
  66.3 20.9 %all-to-all-start.3 = ((f32[16,32,512]{2,1,0:T(8,128)}), f32[16,32,512]{2,1,0:T(8,128)}, u32[]{:S(2)}, u32[]{:S(2)}) async-start(f32[16,32,512]{2,1,0:T(8,128)} %convolution_bitcast_fusion), calls=%async_computation.3 | async-start | bytes 2097152 | tf_op jit(solution)/shard_map/all_to_all | solution.py:47
  73.3 1.4 copy-start
  87.2 61.0 %all-to-all-start.4 = ((bf16[16,2,32776]{2,1,0:T(2,128)(2,1)}), bf16[16,2,32776]{2,1,0:T(2,128)(2,1)S(1)}, u32[]{:S(2)}, u32[]{:S(2)}) async-start(bf16[16,2,32776]{2,1,0:T(2,128)(2,1)} %reshape.209), calls=%async_computation.4 | async-start | bytes 4210688 | tf_op jit(solution)/shard_map/all_to_all | solution.py:29
